TPU v7x, 32 devices: a whole 2x2x4 slice. The times are simulated.
32 devices in a mesh: ma: 8 (over y, x, core), lev: 4 (over z).
Axes of the slice: x: 2, y: 2, z: 4, core: 2. Of those that a mesh axis runs over, the one named last changes fastest.
Arguments:
- spectral_state: float32 [1280, 2, 16, 1280], P('ma', None, None, 'lev'), may hold values from -6 to 6
- forcing_noise: bfloat16 [1280, 2, 16, 1280], P('ma', None, None, 'lev'), may hold values from -6 to 6
- decay_rate: float32 [16], replicated, may hold values from 0.3 to 0.95
- amplitude: float32 [1280], P('lev'), may hold values from 0.2 to 2
- legendre: bfloat16 [1280, 1280, 640], P('ma', 'lev'), may hold values from -0.0048828125 to 0.0048828125
- wave_of_slot: int32 [1280], replicated, may hold values from 0 to 1279, each once
- lat_of_row: int32 [1280], replicated, may hold values from 0 to 1279, each once
Outputs:
- new_state: float32 [1280, 2, 16, 1280], P('ma', None, None, 'lev')
- pattern: bfloat16 [16, 1280, 2560], P('lev', 'ma')
Inputs may be any that keep to these rules, and one draw needn't show every extreme that they name: `wave_of_slot`: each zonal wavenumber is held by exactly one slot. `lat_of_row`: each latitude is held by exactly one row.
All inputs are finite; a program needn't handle non-finite values.
Results may differ from a plain program's by a relative error of at most 0.014.
Values may be sent and summed in bfloat16 or wider, within the bound.
A program may use at most 192 MiB of HBM per device.

v0:
```python
import functools
import math

import jax
import jax.numpy as jnp
from jax import lax
from jax.experimental import pallas as pl
from jax.experimental.pallas import tpu as pltpu
from jax.sharding import PartitionSpec as P

BATCH = 8
LAG = 1
LANES = 128
f32 = jnp.float32
bf16 = jnp.bfloat16


def row_plan(rows):
    whole = rows // LANES * LANES
    rest = rows - whole
    pad = 0
    if rest:
        pad = 16
        while pad < rest:
            pad *= 2
    return whole, rest, pad


def ring_of(lev_size):
    return lev_size + LAG + 2


def table(steps, width):
    steps = jnp.abs(steps - width * jnp.floor(steps * (1.0 / width)))
    steps = jnp.minimum(steps, width - steps)
    near = jnp.minimum(steps, width / 2 - steps)
    angle = near * (2.0 * math.pi / width)
    square = angle * angle
    value = f32(1.0 / math.factorial(12))
    for order in (10, 8, 6, 4, 2, 0):
        value = value * square + (-1.0) ** (order // 2) / math.factorial(order)
    return jnp.where(steps > width / 4, -value, value)


def kernel(dims, state, noise, legendre, decay, amplitude, waves, source, wave_rows, pattern,
           states, noises, weights, own, down, up, total, pick, gathered, outbox, inbox, turned, basis, acc,
           weight_sem, state_sem, noise_sem, down_send, up_send, down_recv, up_recv, box_send, box_recv):
    ma_size, lev_size, chunks, levels, rows, half, width, pair = dims
    me = lax.axis_index("ma")
    z = lax.axis_index("lev")
    top = lev_size - 1
    tall = BATCH * 4 * levels
    whole, rest, pad = row_plan(rows)
    columns = whole + (LANES if rest else 0)
    RING = ring_of(lev_size)
    slots = chunks * BATCH
    width_n = states.shape[-1]
    level_count = levels * lev_size
    far = LAG + jnp.maximum(z, top - z)

    def fetch(c, action):
        slot = lax.rem(c, 2)
        first = c * BATCH
        for src, dst, sem in ((legendre, weights, weight_sem), (state, states, state_sem),
                              (noise, noises, noise_sem)):
            copy = pltpu.make_async_copy(src.at[pl.ds(first, BATCH)], dst.at[slot], sem.at[slot])
            getattr(copy, action)()

    def send_down(c, g):
        slot = lax.rem(c, RING)
        return pltpu.make_async_remote_copy(
            src_ref=own.at[slot, g], dst_ref=down.at[c, g], send_sem=down_send.at[slot, g],
            recv_sem=down_recv.at[c, g], device_id={"lev": z - 1}, device_id_type=pl.DeviceIdType.MESH)

    def send_up(c, g):
        slot = lax.rem(c, RING)
        return pltpu.make_async_remote_copy(
            src_ref=own.at[slot, g], dst_ref=up.at[c, g - 1], send_sem=up_send.at[slot, g - 1],
            recv_sem=up_recv.at[c, g - 1], device_id={"lev": z + 1}, device_id_type=pl.DeviceIdType.MESH)

    def send_box(c, step):
        slot = lax.rem(c, 2)
        other = lax.rem(me + step, ma_size)
        return pltpu.make_async_remote_copy(
            src_ref=outbox.at[slot, other], dst_ref=inbox.at[c, me], send_sem=box_send.at[slot, step - 1],
            recv_sem=box_recv.at[c, step - 1], device_id={"ma": other}, device_id_type=pl.DeviceIdType.MESH)

    def recv_box(c, step):
        other = lax.rem(me + ma_size - step, ma_size)
        return pltpu.make_async_remote_copy(
            src_ref=outbox.at[0, me], dst_ref=inbox.at[c, other], send_sem=box_send.at[0, step - 1],
            recv_sem=box_recv.at[c, step - 1], device_id={"ma": other}, device_id_type=pl.DeviceIdType.MESH)

    def wait_sent(c):
        for g in range(top):
            @pl.when(g < z)
            def _():
                send_down(c, g).wait_send()
        for g in range(1, lev_size):
            @pl.when(g > z)
            def _():
                send_up(c, g).wait_send()

    def partial_sums(c):
        slot = lax.rem(c, 2)
        ring = lax.rem(c, RING)

        place = z * width_n + lax.broadcasted_iota(jnp.int32, (2 * level_count, width_n), 1)

        def one(s, carry):
            offset = place - waves[me * slots + c * BATCH + s]
            value = decay[:, 0:1] * states[slot, s].reshape(2 * level_count, width_n) + amplitude[...] * noises[
                slot, s].reshape(2 * level_count, width_n).astype(f32)
            value = jnp.where(offset >= 0, value, 0.0)
            odd = (offset[0:2 * levels] & 1) == 1
            parts = []
            for g in range(lev_size):
                even = jnp.concatenate([value[g * levels:(g + 1) * levels], value[
                    level_count + g * levels:level_count + (g + 1) * levels]], axis=0)
                parts += [even, jnp.where(odd, -even, even)]
            coef = jnp.concatenate(parts, axis=0).astype(bf16)
            product = jnp.dot(coef, weights[slot, s], preferred_element_type=f32)
            product = product.reshape(lev_size, 4 * levels, half)
            for g in range(lev_size):
                own[ring, g, pl.ds(pl.multiple_of(s * 4 * levels, 16), 4 * levels), :] = product[g].astype(bf16)
            return carry

        lax.fori_loop(0, BATCH, one, 0, unroll=4)

    def add(ring, g, arrived):
        own[ring, g] = (own[ring, g].astype(f32) + arrived.astype(f32)).astype(bf16)

    def pass_down(c):
        ring = lax.rem(c, RING)
        for g in range(top):
            @pl.when(g <= z)
            def _():
                send_down(c, g).wait_recv()

            @pl.when(g < z)
            def _():
                add(ring, g, down[c, g])
                send_down(c, g).start()

    def pass_up(c):
        ring = lax.rem(c, RING)
        for g in range(top, 0, -1):
            @pl.when(g >= z)
            def _():
                send_up(c, g).wait_recv()

            @pl.when(g > z)
            def _():
                add(ring, g, up[c, g - 1])
                send_up(c, g).start()

    def gather(c):
        total[...] = own[lax.rem(c, RING), z].astype(f32)

        @pl.when(z < top)
        def _():
            total[...] += down[c, z].astype(f32)

        @pl.when(z > 0)
        def _():
            total[...] += up[c, z - 1].astype(f32)

    def exchange(c):
        slot = lax.rem(c, 2)

        @pl.when(c >= 2)
        def _():
            for step in range(1, ma_size):
                send_box(c - 2, step).wait_send()

        parts = total[...].reshape(BATCH, 2, 2 * levels, half)
        flat = jnp.concatenate([parts[:, 0].reshape(-1, half), parts[:, 1].reshape(-1, half)], axis=1).astype(bf16)
        for step in range(ma_size):
            other = lax.rem(me + step, ma_size)
            rows_of = jnp.dot(flat, pick[other], preferred_element_type=f32)
            for t in range(columns // LANES):
                gathered[t] = rows_of[:, t * LANES:(t + 1) * LANES]

            def put(lanes, value):
                if step:
                    outbox[slot, other, :, lanes] = value.astype(bf16)
                else:
                    inbox[c, me, :, lanes] = value.astype(bf16)

            for l in range(levels):
                for t in range(whole // LANES):
                    put(pl.ds(l * whole + t * LANES, LANES), gathered[t, pl.ds(l, 2 * BATCH, stride=levels), :])
            if rest:
                each = LANES // pad
                lane = lax.broadcasted_iota(jnp.int32, (2 * BATCH, LANES), 1) // pad
                for first in range(0, levels, each):
                    mixed = None
                    for l in range(first, min(first + each, levels)):
                        value = gathered[whole // LANES, pl.ds(l, 2 * BATCH, stride=levels), :]
                        mixed = value if mixed is None else jnp.where(lane == l - first, value, mixed)
                    put(pl.ds(levels * whole + first * pad, LANES), mixed)
            if step:
                send_box(c, step).start()

    def transform(c):
        depth = ma_size * 2 * BATCH
        first = (c - (pair - 1)) * depth
        deep = pl.ds(pl.multiple_of(first, 256), pair * depth)
        wave = wave_rows[deep, :]
        lane = lax.broadcasted_iota(jnp.int32, wave.shape, 1).astype(f32)
        part = (lax.broadcasted_iota(jnp.int32, wave.shape, 0) & 1).astype(f32)
        factor = jnp.where(wave == 0.0, 1.0, 2.0)
        fine = wave * lane
        fine_cos, fine_sin = table(fine, width), table(fine - width // 4, width)
        rough = wave * (lane * LANES) + part * (width // 4)
        coarse_cos, coarse_sin = factor * table(rough, width), factor * table(rough - width // 4, width)
        blocks = width // LANES
        for a in range(blocks):
            value = coarse_cos[:, a:a + 1] * fine_cos - coarse_sin[:, a:a + 1] * fine_sin
            basis[:, a * LANES:(a + 1) * LANES] = value.astype(bf16)
        for k in range(pair):
            for step in range(1, ma_size):
                recv_box(c - (pair - 1) + k, step).wait_recv()
        spread = inbox[pl.ds(c - (pair - 1), pair)]
        turned[...] = jnp.transpose(spread.reshape(pair * depth, spread.shape[-1]))

        def one(n, carry):
            lanes = pl.ds(pl.multiple_of(n * 256, 256), 256)
            acc[:, lanes] += jnp.dot(turned[...], basis[:, lanes], preferred_element_type=f32)
            return carry

        lax.fori_loop(0, width // 256, one, 0)

    barrier = pltpu.get_barrier_semaphore()
    for step in range(1, ma_size):
        pl.semaphore_signal(barrier, inc=1, device_id={"ma": lax.rem(me + step, ma_size)},
                            device_id_type=pl.DeviceIdType.MESH)

    @pl.when(z > 0)
    def _():
        pl.semaphore_signal(barrier, inc=1, device_id={"lev": z - 1}, device_id_type=pl.DeviceIdType.MESH)

    @pl.when(z < top)
    def _():
        pl.semaphore_signal(barrier, inc=1, device_id={"lev": z + 1}, device_id_type=pl.DeviceIdType.MESH)

    fetch(0, "start")
    inner = (z > 0) & (z < top)

    @pl.when(inner)
    def _():
        pl.semaphore_wait(barrier, ma_size + 1)

    @pl.when(jnp.logical_not(inner))
    def _():
        pl.semaphore_wait(barrier, ma_size)

    def step(i, carry):
        @pl.when(i < chunks)
        def _():
            @pl.when(i + 1 < chunks)
            def _():
                fetch(i + 1, "start")

            fetch(i, "wait")

            @pl.when(i >= RING)
            def _():
                wait_sent(i - RING)

            partial_sums(i)

            @pl.when(z == top)
            def _():
                for g in range(top):
                    send_down(i, g).start()

            @pl.when(z == 0)
            def _():
                for g in range(top, 0, -1):
                    send_up(i, g).start()

        @pl.when(i == 0)
        def _():
            acc[...] = jnp.zeros_like(acc)
            row = lax.broadcasted_iota(jnp.int32, (2 * half, columns), 0)
            for j in range(ma_size):
                pick[j] = jnp.where(row == source[:, j * columns:(j + 1) * columns], 1.0, 0.0).astype(bf16)

        def stage(lag, active, work):
            c = i - lag

            @pl.when((c >= 0) & (c < chunks) & active)
            def _():
                work(c)

        stage(LAG + top - z, z < top, pass_down)
        stage(LAG + z, z > 0, pass_up)
        stage(far, z >= 0, gather)
        stage(far, z >= 0, exchange)
        stage(far + 1, lax.rem(i - far - 1 + pair, pair) == pair - 1, transform)
        return carry

    lax.fori_loop(0, chunks + LAG + top + 1, step, 0)
    for c in range(max(0, chunks - RING), chunks):
        wait_sent(c)
    for c in range(max(0, chunks - 2), chunks):
        for s in range(1, ma_size):
            send_box(c, s).wait_send()
    for l in range(levels):
        if whole:
            pattern[l, 0:whole, :] = acc[l * whole:(l + 1) * whole, :].astype(bf16)
        if rest:
            first = levels * whole + l * pad
            pattern[l, whole:rows, :] = acc[first:first + rest, :].astype(bf16)


def make_body(ma_size, lev_size):
    def body(spectral_state, forcing_noise, decay_rate, amplitude, legendre, wave_of_slot, lat_of_row):
        slot_count, _, level_count, width_n = spectral_state.shape
        levels = level_count // lev_size
        half = legendre.shape[2]
        lat_count = lat_of_row.shape[0]
        width = 2 * lat_count
        rows = lat_count // ma_size
        chunks = slot_count // BATCH
        lev = lax.axis_index("lev")
        wavenum = lax.dynamic_slice_in_dim(wave_of_slot, lax.axis_index("ma") * slot_count, slot_count)
        total_n = lev * width_n + jnp.arange(width_n, dtype=jnp.int32)
        offset = total_n[None, :] - wavenum[:, None]
        updated = decay_rate[None, None, :, None] * spectral_state + amplitude[
            None, None, None, :
        ] * forcing_noise.astype(f32)
        new_state = jnp.where((offset >= 0)[:, None, None, :], updated, f32(0.0))
        whole, rest, pad = row_plan(rows)
        source = jnp.where(lat_of_row < half, lat_of_row, half + lat_count - 1 - lat_of_row)
        source = source.astype(jnp.int32).reshape(ma_size, rows)
        if rest:
            tail = jnp.pad(source[:, whole:], ((0, 0), (0, pad - rest)), constant_values=-1)
            source = jnp.concatenate([source[:, :whole], jnp.tile(tail, (1, LANES // pad))], axis=1)
        columns = source.shape[1]
        wave_rows = wave_of_slot.astype(f32).reshape(ma_size, chunks, BATCH).transpose(1, 0, 2).reshape(-1)
        wave_rows = jnp.broadcast_to(jnp.repeat(wave_rows, 2)[:, None], (2 * wave_rows.shape[0], LANES))
        decay = jnp.broadcast_to(jnp.tile(decay_rate, 2)[:, None], (2 * level_count, LANES))
        depth = ma_size * 2 * BATCH
        pair = max(1, 256 // depth)
        spread = levels * (whole + pad)
        tall = BATCH * 4 * levels
        dims = (ma_size, lev_size, chunks, levels, rows, half, width, pair)
        any_space = pl.BlockSpec(memory_space=pl.ANY)
        vmem = pl.BlockSpec(memory_space=pltpu.VMEM)
        dma = pltpu.SemaphoreType.DMA
        pattern = pl.pallas_call(
            functools.partial(kernel, dims),
            out_shape=jax.ShapeDtypeStruct((levels, rows, width), bf16),
            in_specs=[any_space, any_space, any_space, vmem, vmem, pl.BlockSpec(memory_space=pltpu.SMEM), vmem, vmem],
            out_specs=vmem,
            scratch_shapes=[
                pltpu.VMEM((2, BATCH, 2, level_count, width_n), f32),
                pltpu.VMEM((2, BATCH, 2, level_count, width_n), bf16),
                pltpu.VMEM((2, BATCH, width_n, half), bf16),
                pltpu.VMEM((ring_of(lev_size), lev_size, tall, half), bf16),
                pltpu.VMEM((chunks, lev_size - 1, tall, half), bf16),
                pltpu.VMEM((chunks, lev_size - 1, tall, half), bf16),
                pltpu.VMEM((tall, half), f32),
                pltpu.VMEM((ma_size, 2 * half, columns), bf16),
                pltpu.VMEM((columns // LANES, BATCH * 2 * levels, LANES), f32),
                pltpu.VMEM((2, ma_size, 2 * BATCH, spread), bf16),
                pltpu.VMEM((chunks, ma_size, 2 * BATCH, spread), bf16),
                pltpu.VMEM((spread, pair * depth), bf16),
                pltpu.VMEM((pair * depth, width), bf16),
                pltpu.VMEM((spread, width), f32),
                dma((2,)), dma((2,)), dma((2,)),
                dma((ring_of(lev_size), lev_size - 1)), dma((ring_of(lev_size), lev_size - 1)),
                dma((chunks, lev_size - 1)), dma((chunks, lev_size - 1)),
                dma((2, ma_size - 1)), dma((chunks, ma_size - 1)),
            ],
            compiler_params=pltpu.CompilerParams(
                collective_id=0, has_side_effects=True, vmem_limit_bytes=64 * 1024 * 1024 - 65536),
        )(spectral_state, forcing_noise, legendre, decay, amplitude.reshape(1, -1), wave_of_slot.astype(jnp.int32),
          source.reshape(1, -1), wave_rows)
        return (new_state, pattern)

    return body


def solution(mesh):
    return jax.shard_map(
        make_body(mesh.shape["ma"], mesh.shape["lev"]),
        mesh=mesh,
        in_specs=(
            P("ma", None, None, "lev"),
            P("ma", None, None, "lev"),
            P(),
            P("lev"),
            P("ma", "lev", None),
            P(),
            P(),
        ),
        out_specs=(P("ma", None, None, "lev"), P("lev", "ma", None)),
        check_vma=False,
    )
```

profile of v0, /device:TPU:0, one launch (start us, length us, event | category | flops | bytes accessed | tf_op | source)
XLA Modules:
  0.0 263.7 jit_solution(4005349694791944765)
XLA Ops:
  0.6 0.8 dynamic_slice.3
  1.4 0.7 tile.6
  2.1 0.1 broadcast_in_dim.36
  2.2 1.2 reshape.56.amplitude
  3.4 0.7 compare_select_fusion
  4.1 0.1 reshape.57
  4.2 0.7 convert_element_type.7
  4.9 0.1 tile.8
  5.0 0.6 copy.10
  5.6 0.7 broadcast_in_dim.37.decay
  6.2 0.7 subtract_compare_fusion
  7.0 0.1 reshape.59
  7.1 0.1 reshape.60
  7.2 0.2 broadcast_in_dim.38
  7.4 0.3 broadcast_in_dim.39
  7.8 1.5 broadcast_in_dim.40.wave_rows
  9.2 242.9 %shard_map.86 = bf16[4,160,2560]{2,1,0:T(8,128)(2,1)} custom-call(f32[160,2,16,320]{3,2,1,0:T(8,128)} %state.1, bf16[160,2,16,320]{3,2,1,0:T(8,128)(2,1)} %noise.1, bf16[160,320,640]{2,1,0:T(8,128)(2,1)} %legendre.1, f32[32,128]{1,0:T(8,128)} %broadcast_in_dim.37.decay, f32[1,320]{1,0:T(1,128)} %reshape.56.amplitude, s32[1280]{0:T(1024)} %waves.1, ...), custom_call_target="tpu_custom_call" | custom-call | tf_op jit(solution)/shard_map/pallas_call | solution.py:353
  252.1 0.0 copy-start
  252.1 9.9 %add_select_fusion = f32[160,2,16,320]{3,2,1,0:T(8,128)} fusion(bf16[160,2,16,320]{3,2,1,0:T(8,128)(2,1)} %noise.1, f32[160,2,16,320]{3,2,1,0:T(8,128)} %state.1, f32[320]{0:T(512)} %param.10, f32[16]{0:T(128)} %param.9, pred[160,320]{1,0:T(8,128)(4,1)} %subtract_compare_fusion), kind=kLoop, calls=%fused_computation | loop fusion | flops 8192000 | bytes 16436544 | tf_op jit(solution)/shard_map/jit(_where)/select_n | solution.py:334
  262.0 0.0 copy-done
  262.0 1.7 copy.12
  (6 shorter events, 0.0 us)
Async XLA Ops:
  252.1 9.9 %copy-start = (bf16[4,160,2560]{2,1,0:T(8,128)(2,1)S(1)}, bf16[4,160,2560]{2,1,0:T(8,128)(2,1)}, u32[]{:S(2)}) copy-start(bf16[4,160,2560]{2,1,0:T(8,128)(2,1)} %shard_map.86) | copy-start | bytes 9830404
where the time goes:
time: 264 us
  Pallas kernels  243 us (92%)
  other arithmetic  12 us (5%)
  local copies, waits for them, and re-layouts  8.13 us (3%)
    pallas_call x1, Pallas kernels, body(): pl.pallas_call(functools.partial(kernel, dims), out_shape=jax.ShapeDtypeS...  243 us
    select_n x1, other arithmetic, body(): new_state = jnp.where((offset >= 0)[:, None, None, :], updated, f32(0.0))  9.88 us

commit v1 on v0

v1 whole, which is shorter than its diff:
```python
import functools
import math

import jax
import jax.numpy as jnp
from jax import lax
from jax.experimental import pallas as pl
from jax.experimental.pallas import tpu as pltpu
from jax.sharding import PartitionSpec as P

BATCH = 8
SPARE = 3 * 1024 * 1024
LAG = 1
LANES = 128
f32 = jnp.float32
bf16 = jnp.bfloat16


def row_plan(rows):
    whole = rows // LANES * LANES
    rest = rows - whole
    pad = 0
    if rest:
        pad = 16
        while pad < rest:
            pad *= 2
    return whole, rest, pad


def ring_of(lev_size):
    return lev_size + LAG + 2


def table(steps, width):
    steps = jnp.abs(steps - width * jnp.floor(steps * (1.0 / width)))
    steps = jnp.minimum(steps, width - steps)
    near = jnp.minimum(steps, width / 2 - steps)
    angle = near * (2.0 * math.pi / width)
    square = angle * angle
    value = f32(1.0 / math.factorial(12))
    for order in (10, 8, 6, 4, 2, 0):
        value = value * square + (-1.0) ** (order // 2) / math.factorial(order)
    return jnp.where(steps > width / 4, -value, value)


def kernel(dims, state, noise, legendre, decay_in, amplitude_in, waves_in, source_in, new_state, pattern,
           decay, amplitude, waves, source, states, noises, fresh, weights, decays, wave_rows, own, arrived, total, pick, gathered, outbox, inbox, turned, basis, acc,
           small_sem, weight_sem, state_sem, noise_sem, fresh_sem, down_send, up_send, down_recv, up_recv, box_send, box_recv):
    ma_size, lev_size, chunks, levels, rows, half, width, pair = dims
    me = lax.axis_index("ma")
    z = lax.axis_index("lev")
    top = lev_size - 1
    tall = BATCH * 4 * levels
    whole, rest, pad = row_plan(rows)
    columns = whole + (LANES if rest else 0)
    RING = ring_of(lev_size)
    slots = chunks * BATCH
    width_n = states.shape[-1]
    level_count = levels * lev_size
    far = LAG + jnp.maximum(z, top - z)

    def fetch(c, action):
        slot = lax.rem(c, 2)
        first = c * BATCH
        for src, dst, sem in ((state, states, state_sem), (noise, noises, noise_sem),
                              (legendre, weights, weight_sem)):
            copy = pltpu.make_async_copy(src.at[pl.ds(first, BATCH)], dst.at[slot], sem.at[slot])
            getattr(copy, action)()

    def store_fresh(c):
        slot = lax.rem(c, 2)
        return pltpu.make_async_copy(fresh.at[slot], new_state.at[pl.ds(c * BATCH, BATCH)], fresh_sem.at[slot])

    def send_down(c, g):
        slot = lax.rem(c, RING)
        return pltpu.make_async_remote_copy(
            src_ref=own.at[slot, g], dst_ref=arrived.at[c, g], send_sem=down_send.at[slot, g],
            recv_sem=down_recv.at[c, g], device_id={"lev": z - 1}, device_id_type=pl.DeviceIdType.MESH)

    def send_up(c, g):
        slot = lax.rem(c, RING)
        return pltpu.make_async_remote_copy(
            src_ref=own.at[slot, g], dst_ref=arrived.at[c, g + 1], send_sem=up_send.at[slot, g - 1],
            recv_sem=up_recv.at[c, g - 1], device_id={"lev": z + 1}, device_id_type=pl.DeviceIdType.MESH)

    def send_box(c, step):
        slot = lax.rem(c, 2)
        other = lax.rem(me + step, ma_size)
        return pltpu.make_async_remote_copy(
            src_ref=outbox.at[slot, other], dst_ref=inbox.at[c, me], send_sem=box_send.at[slot, step - 1],
            recv_sem=box_recv.at[c, step - 1], device_id={"ma": other}, device_id_type=pl.DeviceIdType.MESH)

    def recv_box(c, step):
        other = lax.rem(me + ma_size - step, ma_size)
        return pltpu.make_async_remote_copy(
            src_ref=outbox.at[0, me], dst_ref=inbox.at[c, other], send_sem=box_send.at[0, step - 1],
            recv_sem=box_recv.at[c, step - 1], device_id={"ma": other}, device_id_type=pl.DeviceIdType.MESH)

    def wait_sent(c):
        for g in range(top):
            @pl.when(g < z)
            def _():
                send_down(c, g).wait_send()
        for g in range(1, lev_size):
            @pl.when(g > z)
            def _():
                send_up(c, g).wait_send()

    def partial_sums(c):
        slot = lax.rem(c, 2)
        ring = lax.rem(c, RING)

        place = z * width_n + lax.broadcasted_iota(jnp.int32, (2 * level_count, width_n), 1)

        @pl.when(c >= 2)
        def _():
            store_fresh(c - 2).wait()

        def one(s, carry):
            offset = place - waves[me * slots + c * BATCH + s]
            value = decays[:, 0:1] * states[slot, s].reshape(2 * level_count, width_n) + amplitude[...] * noises[
                slot, s].reshape(2 * level_count, width_n).astype(f32)
            value = jnp.where(offset >= 0, value, 0.0)
            fresh[slot, s] = value.reshape(2, level_count, width_n)
            odd = (offset[0:2 * levels] & 1) == 1
            parts = []
            for g in range(lev_size):
                even = jnp.concatenate([value[g * levels:(g + 1) * levels], value[
                    level_count + g * levels:level_count + (g + 1) * levels]], axis=0)
                parts += [even, jnp.where(odd, -even, even)]
            coef = jnp.concatenate(parts, axis=0).astype(bf16)
            product = jnp.dot(coef, weights[slot, s], preferred_element_type=f32)
            product = product.reshape(lev_size, 4 * levels, half)
            for g in range(lev_size):
                own[ring, g, pl.ds(pl.multiple_of(s * 4 * levels, 16), 4 * levels), :] = product[g].astype(bf16)
            return carry

        lax.fori_loop(0, BATCH, one, 0, unroll=4)
        store_fresh(c).start()

    def add(ring, g, value):
        own[ring, g] = (own[ring, g].astype(f32) + value.astype(f32)).astype(bf16)

    def pass_down(c):
        ring = lax.rem(c, RING)
        for g in range(top):
            @pl.when(g < z)
            def _():
                send_down(c, g).wait_recv()
                add(ring, g, arrived[c, g])
                send_down(c, g).start()

    def pass_up(c):
        ring = lax.rem(c, RING)
        for g in range(top, 0, -1):
            @pl.when(g > z)
            def _():
                send_up(c, g).wait_recv()
                add(ring, g, arrived[c, g + 1])
                send_up(c, g).start()

    def gather(c):
        total[...] = own[lax.rem(c, RING), z].astype(f32)

        @pl.when(z < top)
        def _():
            send_down(c, z).wait_recv()
            total[...] += arrived[c, z].astype(f32)

        @pl.when(z > 0)
        def _():
            send_up(c, z).wait_recv()
            total[...] += arrived[c, z + 1].astype(f32)

    def exchange(c):
        slot = lax.rem(c, 2)

        @pl.when(c >= 2)
        def _():
            for step in range(1, ma_size):
                send_box(c - 2, step).wait_send()

        parts = total[...].reshape(BATCH, 2, 2 * levels, half)
        flat = jnp.concatenate([parts[:, 0].reshape(-1, half), parts[:, 1].reshape(-1, half)], axis=1).astype(bf16)
        for first in range(0, ma_size * columns, 1024):
            rows_of = jnp.dot(flat, pick[:, first:first + 1024], preferred_element_type=f32)
            for t in range(1024 // LANES):
                gathered[first // LANES + t] = rows_of[:, t * LANES:(t + 1) * LANES]
        for step in range(ma_size):
            other = lax.rem(me + step, ma_size)
            tile = other * (columns // LANES)

            def put(lanes, value):
                if step:
                    outbox[slot, other, :, lanes] = value.astype(bf16)
                else:
                    inbox[c, me, :, lanes] = value.astype(bf16)

            for l in range(levels):
                for t in range(whole // LANES):
                    put(pl.ds(l * whole + t * LANES, LANES), gathered[tile + t, pl.ds(l, 2 * BATCH, stride=levels), :])
            if rest:
                each = LANES // pad
                lane = lax.broadcasted_iota(jnp.int32, (2 * BATCH, LANES), 1) // pad
                for first in range(0, levels, each):
                    mixed = None
                    for l in range(first, min(first + each, levels)):
                        value = gathered[tile + whole // LANES, pl.ds(l, 2 * BATCH, stride=levels), :]
                        mixed = value if mixed is None else jnp.where(lane == l - first, value, mixed)
                    put(pl.ds(levels * whole + first * pad, LANES), mixed)
            if step:
                send_box(c, step).start()

    depth = ma_size * 2 * BATCH
    held = basis.shape[0]

    def waves_of(c):
        row = lax.broadcasted_iota(jnp.int32, (2 * BATCH, LANES), 0) // 2

        def one(n, carry):
            first = lax.rem(n, ma_size) * slots + (c - (pair - 1) + n // ma_size) * BATCH
            value = jnp.zeros((2 * BATCH, LANES), f32)
            for s in range(BATCH):
                value = jnp.where(row == s, waves[first + s].astype(f32), value)
            wave_rows[pl.ds(pl.multiple_of(n * 2 * BATCH, 2 * BATCH), 2 * BATCH), :] = value
            return carry

        lax.fori_loop(0, pair * ma_size, one, 0)
        wave = wave_rows[...]
        lane = lax.broadcasted_iota(jnp.int32, wave.shape, 1).astype(f32)
        part = (lax.broadcasted_iota(jnp.int32, wave.shape, 0) & 1).astype(f32)
        factor = jnp.where(wave == 0.0, 1.0, 2.0)
        fine = wave * lane
        fine_cos, fine_sin = table(fine, width), table(fine - width // 4, width)
        rough = wave * (lane * LANES) + part * (width // 4)
        coarse_cos, coarse_sin = factor * table(rough, width), factor * table(rough - width // 4, width)
        slot = lax.rem(c // pair, held)
        for a in range(width // LANES):
            value = coarse_cos[:, a:a + 1] * fine_cos - coarse_sin[:, a:a + 1] * fine_sin
            basis[slot, :, a * LANES:(a + 1) * LANES] = value.astype(bf16)

    def turn(c):
        for k in range(pair):
            for step in range(1, ma_size):
                recv_box(c - (pair - 1) + k, step).wait_recv()
        spread = inbox[pl.ds(c - (pair - 1), pair)]
        turned[...] = jnp.transpose(spread.reshape(pair * depth, spread.shape[-1]))

    def transform(c):
        turn(c)

        def one(n, carry):
            lanes = pl.ds(pl.multiple_of(n * 256, 256), 256)
            acc[:, lanes] += jnp.dot(turned[...], basis[lax.rem(c // pair, held), :, lanes], preferred_element_type=f32)
            return carry

        lax.fori_loop(0, width // 256, one, 0)

    def finish(c):
        turn(c)
        for n in range(width // 256):
            lanes = pl.ds(n * 256, 256)
            value = (acc[:, lanes] + jnp.dot(
                turned[...], basis[(c // pair) % held, :, lanes], preferred_element_type=f32)).astype(bf16)
            for l in range(levels):
                if whole:
                    pattern[l, 0:whole, lanes] = value[l * whole:(l + 1) * whole]
                if rest:
                    first = levels * whole + l * pad
                    pattern[l, whole:rows, lanes] = value[first:first + rest]

    barrier = pltpu.get_barrier_semaphore()
    for step in range(1, ma_size):
        pl.semaphore_signal(barrier, inc=1, device_id={"ma": lax.rem(me + step, ma_size)},
                            device_id_type=pl.DeviceIdType.MESH)

    @pl.when(z > 0)
    def _():
        pl.semaphore_signal(barrier, inc=1, device_id={"lev": z - 1}, device_id_type=pl.DeviceIdType.MESH)

    @pl.when(z < top)
    def _():
        pl.semaphore_signal(barrier, inc=1, device_id={"lev": z + 1}, device_id_type=pl.DeviceIdType.MESH)

    small = [pltpu.make_async_copy(src, dst, small_sem.at[n]) for n, (src, dst) in enumerate((
        (decay_in, decay), (amplitude_in, amplitude), (waves_in, waves), (source_in, source)))]
    for copy in small:
        copy.start()
    fetch(0, "start")
    for copy in small:
        copy.wait()
    level = lax.rem(lax.broadcasted_iota(jnp.int32, decays.shape, 0), level_count)
    rate = jnp.zeros(decays.shape, f32)
    for l in range(level_count):
        rate = jnp.where(level == l, decay[l], rate)
    decays[...] = rate
    fetch(0, "wait")
    partial_sums(0)
    inner = (z > 0) & (z < top)

    @pl.when(inner)
    def _():
        pl.semaphore_wait(barrier, ma_size + 1)

    @pl.when(jnp.logical_not(inner))
    def _():
        pl.semaphore_wait(barrier, ma_size)

    def step(i, carry):
        @pl.when(i < chunks)
        def _():
            @pl.when(i + 1 < chunks)
            def _():
                fetch(i + 1, "start")

            @pl.when(i > 0)
            def _():
                fetch(i, "wait")

                @pl.when(i >= RING)
                def _():
                    wait_sent(i - RING)

                partial_sums(i)

            @pl.when(z == top)
            def _():
                for g in range(top - 1):
                    send_down(i, g).start()

                @pl.when(i > 0)
                def _():
                    send_down(i - 1, top - 1).start()

                @pl.when(i == chunks - 1)
                def _():
                    send_down(i, top - 1).start()

            @pl.when(z == 0)
            def _():
                for g in range(top, 1, -1):
                    send_up(i, g).start()

                @pl.when(i > 0)
                def _():
                    send_up(i - 1, 1).start()

                @pl.when(i == chunks - 1)
                def _():
                    send_up(i, 1).start()

        @pl.when(i == 0)
        def _():
            acc[...] = jnp.zeros_like(acc)
            row = lax.broadcasted_iota(jnp.int32, (2 * half, columns), 0)
            for j in range(ma_size):
                pick[:, j * columns:(j + 1) * columns] = jnp.where(row == source[:, j * columns:(j + 1) * columns], 1.0, 0.0).astype(bf16)

        def stage(lag, active, work):
            c = i - lag

            @pl.when((c >= 0) & (c < chunks) & active)
            def _():
                work(c)

        early = far - 2
        stage(early, lax.rem(i - early + pair, pair) == pair - 1, waves_of)
        stage(LAG + top - z, z < top, pass_down)
        stage(LAG + z, z > 0, pass_up)
        stage(far, z >= 0, gather)
        stage(far, z >= 0, exchange)
        stage(far + 1, (lax.rem(i - far - 1 + pair, pair) == pair - 1) & (i - far - 1 < chunks - 1), transform)
        return carry

    lax.fori_loop(0, chunks + LAG + top, step, 0)
    finish(chunks - 1)
    for c in range(max(0, chunks - 2), chunks):
        store_fresh(c).wait()
    for c in range(max(0, chunks - RING), chunks):
        wait_sent(c)
    for c in range(max(0, chunks - 2), chunks):
        for s in range(1, ma_size):
            send_box(c, s).wait_send()


def make_body(ma_size, lev_size):
    def body(spectral_state, forcing_noise, decay_rate, amplitude, legendre, wave_of_slot, lat_of_row):
        slot_count, _, level_count, width_n = spectral_state.shape
        levels = level_count // lev_size
        half = legendre.shape[2]
        lat_count = lat_of_row.shape[0]
        width = 2 * lat_count
        rows = lat_count // ma_size
        chunks = slot_count // BATCH
        whole, rest, pad = row_plan(rows)
        source = jnp.where(lat_of_row < half, lat_of_row, half + lat_count - 1 - lat_of_row)
        source = source.astype(jnp.int32).reshape(ma_size, rows)
        if rest:
            tail = jnp.pad(source[:, whole:], ((0, 0), (0, pad - rest)), constant_values=-1)
            source = jnp.concatenate([source[:, :whole], jnp.tile(tail, (1, LANES // pad))], axis=1)
        columns = source.shape[1]
        depth = ma_size * 2 * BATCH
        pair = max(1, 256 // depth)
        spread = levels * (whole + pad)
        tall = BATCH * 4 * levels
        dims = (ma_size, lev_size, chunks, levels, rows, half, width, pair)
        any_space = pl.BlockSpec(memory_space=pl.ANY)
        vmem = pl.BlockSpec(memory_space=pltpu.VMEM)
        dma = pltpu.SemaphoreType.DMA
        source = source.reshape(1, -1)
        ring = ring_of(lev_size)
        arrays = [
            ((1, width_n), f32), (source.shape, jnp.int32),
            ((2, BATCH, 2, level_count, width_n), f32),
            ((2, BATCH, 2, level_count, width_n), bf16),
            ((2, BATCH, 2, level_count, width_n), f32),
            ((2, BATCH, width_n, half), bf16),
            ((2 * level_count, LANES), f32),
            ((pair * depth, LANES), f32),
            ((ring, lev_size, tall, half), bf16),
            ((chunks, lev_size + 1, tall, half), bf16),
            ((tall, half), f32),
            ((2 * half, ma_size * columns), bf16),
            ((ma_size * columns // LANES, BATCH * 2 * levels, LANES), f32),
            ((2, ma_size, 2 * BATCH, spread), bf16),
            ((chunks, ma_size, 2 * BATCH, spread), bf16),
            ((spread, pair * depth), bf16),
            ((3 // pair + 1, pair * depth, width), bf16),
            ((spread, width), f32),
        ]
        scratch = [pltpu.VMEM(shape, kind) for shape, kind in arrays]
        bytes_held = sum(math.prod(shape[:-1]) * -(-shape[-1] // LANES) * LANES * jnp.dtype(kind).itemsize
                         for shape, kind in arrays)
        smem = pltpu.SMEM
        return pl.pallas_call(
            functools.partial(kernel, dims),
            out_shape=(jax.ShapeDtypeStruct(spectral_state.shape, f32),
                       jax.ShapeDtypeStruct((levels, rows, width), bf16)),
            in_specs=[any_space, any_space, any_space] + [pl.BlockSpec(memory_space=pltpu.HBM)] * 4,
            out_specs=(any_space, vmem),
            scratch_shapes=[
                smem(decay_rate.shape, f32), scratch[0], smem(wave_of_slot.shape, jnp.int32), *scratch[1:],
                dma((4,)),
                dma((2,)), dma((2,)), dma((2,)), dma((2,)),
                dma((ring, lev_size - 1)), dma((ring, lev_size - 1)),
                dma((chunks, lev_size - 1)), dma((chunks, lev_size - 1)),
                dma((2, ma_size - 1)), dma((chunks, ma_size - 1)),
            ],
            compiler_params=pltpu.CompilerParams(
                collective_id=0, has_side_effects=True, vmem_limit_bytes=min(bytes_held + SPARE, 67043328)),
        )(spectral_state, forcing_noise, legendre, decay_rate, amplitude.reshape(1, -1), wave_of_slot.astype(jnp.int32), source)

    return body


def solution(mesh):
    return jax.shard_map(
        make_body(mesh.shape["ma"], mesh.shape["lev"]),
        mesh=mesh,
        in_specs=(
            P("ma", None, None, "lev"),
            P("ma", None, None, "lev"),
            P(),
            P("lev"),
            P("ma", "lev", None),
            P(),
            P(),
        ),
        out_specs=(P("ma", None, None, "lev"), P("lev", "ma", None)),
        check_vma=False,
    )
```

time: 264 us -> 245 us (0.928)
  other arithmetic: 12 us -> 0.7 us
  Pallas kernels: 243 us -> 232 us
  local copies, waits for them, and re-layouts: 8.13 us -> 11.1 us
    pallas_call x1, Pallas kernels: 243 us -> 232 us  [body(): pl.pallas_call(functools.partial(kernel, dims), out_shape=(jax.ShapeDtype...]
    select_n x1 -> x0, other arithmetic: 9.88 us -> none  [body(): new_state = jnp.where((offset >= 0)[:, None, None, :], updated, f32(0.0))]
    unnamed x4 -> x7, local copies, waits for them, and re-layouts: 2.32 us -> 10.2 us
    broadcast_in_dim x5 -> x0, local copies, waits for them, and re-layouts: 2.77 us -> none  [the longest x2 1.79 us: body(): jnp.broadcast_to(jnp.repeat(wave_rows, 2)[:, None], (2 * wave_rows.shape[...]
where the time goes in v1:
time: 245 us
  Pallas kernels  232 us (95%)
  local copies, waits for them, and re-layouts  11.1 us (5%)
    pallas_call x1, Pallas kernels, body(): pl.pallas_call(functools.partial(kernel, dims), out_shape=(jax.ShapeDtype...  232 us
    unnamed x7, local copies, waits for them, and re-layouts  10.2 us

profile of v1, /device:TPU:0, one launch (start us, length us, event | category | flops | bytes accessed | tf_op | source)
XLA Modules:
  0.0 244.6 jit_solution(15542976029200816395)
XLA Ops:
  0.6 0.7 reshape.17.amplitude_in
  1.3 0.7 compare_select_fusion
  2.0 0.1 reshape.18
  2.1 0.1 tile.10
  2.2 0.0 copy-start
  2.2 0.7 copy-done
  2.9 0.0 copy-start.1
  2.9 0.7 copy-done.1
  3.6 232.1 %shard_map.86 = (f32[160,2,16,320]{3,2,1,0:T(8,128)}, bf16[4,160,2560]{2,1,0:T(8,128)(2,1)S(1)}) custom-call(f32[160,2,16,320]{3,2,1,0:T(8,128)} %state.1, bf16[160,2,16,320]{3,2,1,0:T(8,128)(2,1)} %noise.1, bf16[160,320,640]{2,1,0:T(8,128)(2,1)} %legendre.1, f32[16]{0:T(128)S(1)} %copy-done.1, f32[1,320]{1,0:T(1,128)S(1)} %reshape.17.amplitude_in, ...), custom_call_target="tpu_custom_call" | custom-call | tf_op jit(solution)/shard_map/pallas_call | solution.py:435
  235.7 7.2 %copy.12 = f32[160,2,16,320]{3,2,1,0:T(8,128)} copy(f32[160,2,16,320]{3,2,1,0:T(8,128)} %get-tuple-element.4) | data formatting | bytes 13107200
  242.9 1.7 copy.13
  (5 shorter events, 0.0 us)
Async XLA Ops:
  2.2 0.7 copy-start
  2.9 0.7 copy-start.1

commit v2 on v1

--- a/solution.py
+++ b/solution.py
@@ -9,6 +9,7 @@
 from jax.sharding import PartitionSpec as P
 
 BATCH = 8
+PIECES = 8
 SPARE = 3 * 1024 * 1024
 LAG = 1
 LANES = 128
@@ -43,7 +44,7 @@
     return jnp.where(steps > width / 4, -value, value)
 
 
-def kernel(dims, state, noise, legendre, decay_in, amplitude_in, waves_in, source_in, new_state, pattern,
+def kernel(dims, state, noise, legendre, small_in, source_in, new_state, pattern,
            decay, amplitude, waves, source, states, noises, fresh, weights, decays, wave_rows, own, arrived, total, pick, gathered, outbox, inbox, turned, basis, acc,
            small_sem, weight_sem, state_sem, noise_sem, fresh_sem, down_send, up_send, down_recv, up_recv, box_send, box_recv):
     ma_size, lev_size, chunks, levels, rows, half, width, pair = dims
@@ -111,18 +112,19 @@
         ring = lax.rem(c, RING)
 
         place = z * width_n + lax.broadcasted_iota(jnp.int32, (2 * level_count, width_n), 1)
+        place = place.astype(f32)
 
         @pl.when(c >= 2)
         def _():
             store_fresh(c - 2).wait()
 
         def one(s, carry):
-            offset = place - waves[me * slots + c * BATCH + s]
-            value = decays[:, 0:1] * states[slot, s].reshape(2 * level_count, width_n) + amplitude[...] * noises[
+            offset = place - waves[0, me * slots + c * BATCH + s]
+            value = decays[:, 0:1] * states[slot, s].reshape(2 * level_count, width_n) + amplitude[:, 0:width_n] * noises[
                 slot, s].reshape(2 * level_count, width_n).astype(f32)
             value = jnp.where(offset >= 0, value, 0.0)
             fresh[slot, s] = value.reshape(2, level_count, width_n)
-            odd = (offset[0:2 * levels] & 1) == 1
+            odd = (offset[0:2 * levels].astype(jnp.int32) & 1) == 1
             parts = []
             for g in range(lev_size):
                 even = jnp.concatenate([value[g * levels:(g + 1) * levels], value[
@@ -221,7 +223,7 @@
             first = lax.rem(n, ma_size) * slots + (c - (pair - 1) + n // ma_size) * BATCH
             value = jnp.zeros((2 * BATCH, LANES), f32)
             for s in range(BATCH):
-                value = jnp.where(row == s, waves[first + s].astype(f32), value)
+                value = jnp.where(row == s, waves[0, first + s], value)
             wave_rows[pl.ds(pl.multiple_of(n * 2 * BATCH, 2 * BATCH), 2 * BATCH), :] = value
             return carry
 
@@ -283,7 +285,9 @@
         pl.semaphore_signal(barrier, inc=1, device_id={"lev": z + 1}, device_id_type=pl.DeviceIdType.MESH)
 
     small = [pltpu.make_async_copy(src, dst, small_sem.at[n]) for n, (src, dst) in enumerate((
-        (decay_in, decay), (amplitude_in, amplitude), (waves_in, waves), (source_in, source)))]
+        (small_in.at[:, pl.ds(0, waves.shape[1])], waves),
+        (small_in.at[:, pl.ds(waves.shape[1], amplitude.shape[1])], amplitude),
+        (small_in.at[:, pl.ds(waves.shape[1] + amplitude.shape[1], LANES)], decay), (source_in, source)))]
     for copy in small:
         copy.start()
     fetch(0, "start")
@@ -292,7 +296,7 @@
     level = lax.rem(lax.broadcasted_iota(jnp.int32, decays.shape, 0), level_count)
     rate = jnp.zeros(decays.shape, f32)
     for l in range(level_count):
-        rate = jnp.where(level == l, decay[l], rate)
+        rate = jnp.where(level == l, decay[0, l], rate)
     decays[...] = rate
     fetch(0, "wait")
     partial_sums(0)
@@ -381,6 +385,17 @@
     for c in range(max(0, chunks - 2), chunks):
         for s in range(1, ma_size):
             send_box(c, s).wait_send()
+
+
+def deliver(made_state, made_pattern, new_state, pattern, sems):
+    piece = made_state.shape[0] // PIECES
+    copies = [pltpu.make_async_copy(made_state.at[pl.ds(n * piece, piece)], new_state.at[pl.ds(n * piece, piece)],
+                                    sems.at[n]) for n in range(PIECES)]
+    copies.append(pltpu.make_async_copy(made_pattern, pattern, sems.at[PIECES]))
+    for copy in copies:
+        copy.start()
+    for copy in copies:
+        copy.wait()
 
 
 def make_body(ma_size, lev_size):
@@ -408,9 +423,11 @@
         vmem = pl.BlockSpec(memory_space=pltpu.VMEM)
         dma = pltpu.SemaphoreType.DMA
         source = source.reshape(1, -1)
+        small = jnp.concatenate([
+            wave_of_slot.astype(f32), jnp.pad(amplitude, (0, -width_n % LANES)), jnp.pad(decay_rate, (0, LANES - level_count))])
         ring = ring_of(lev_size)
         arrays = [
-            ((1, width_n), f32), (source.shape, jnp.int32),
+            ((1, -(-width_n // LANES) * LANES), f32), (source.shape, jnp.int32),
             ((2, BATCH, 2, level_count, width_n), f32),
             ((2, BATCH, 2, level_count, width_n), bf16),
             ((2, BATCH, 2, level_count, width_n), f32),
@@ -432,14 +449,14 @@
         bytes_held = sum(math.prod(shape[:-1]) * -(-shape[-1] // LANES) * LANES * jnp.dtype(kind).itemsize
                          for shape, kind in arrays)
         smem = pltpu.SMEM
-        return pl.pallas_call(
+        made = pl.pallas_call(
             functools.partial(kernel, dims),
             out_shape=(jax.ShapeDtypeStruct(spectral_state.shape, f32),
                        jax.ShapeDtypeStruct((levels, rows, width), bf16)),
-            in_specs=[any_space, any_space, any_space] + [pl.BlockSpec(memory_space=pltpu.HBM)] * 4,
+            in_specs=[any_space, any_space, any_space] + [any_space] * 2,
             out_specs=(any_space, vmem),
             scratch_shapes=[
-                smem(decay_rate.shape, f32), scratch[0], smem(wave_of_slot.shape, jnp.int32), *scratch[1:],
+                smem((1, LANES), f32), scratch[0], smem((1, wave_of_slot.shape[0]), f32), *scratch[1:],
                 dma((4,)),
                 dma((2,)), dma((2,)), dma((2,)), dma((2,)),
                 dma((ring, lev_size - 1)), dma((ring, lev_size - 1)),
@@ -448,7 +465,16 @@
             ],
             compiler_params=pltpu.CompilerParams(
                 collective_id=0, has_side_effects=True, vmem_limit_bytes=min(bytes_held + SPARE, 67043328)),
-        )(spectral_state, forcing_noise, legendre, decay_rate, amplitude.reshape(1, -1), wave_of_slot.astype(jnp.int32), source)
+        )(spectral_state, forcing_noise, legendre, small.reshape(1, -1), source)
+        return pl.pallas_call(
+            deliver,
+            out_shape=(jax.ShapeDtypeStruct(spectral_state.shape, f32),
+                       jax.ShapeDtypeStruct((levels, rows, width), bf16)),
+            in_specs=[vmem, vmem],
+            out_specs=(any_space, any_space),
+            scratch_shapes=[dma((PIECES + 1,))],
+            compiler_params=pltpu.CompilerParams(vmem_limit_bytes=16 * 1024 * 1024),
+        )(*made)
 
     return body
 

time: 245 us -> 243 us (level)
  local copies, waits for them, and re-layouts: 11.1 us -> 3.41 us
  Pallas kernels: 232 us -> 237 us
    unnamed x7 -> x3, local copies, waits for them, and re-layouts: 10.2 us -> 3.24 us
    pallas_call x0 -> x1, Pallas kernels: none -> 4.29 us  [body(): pl.pallas_call(deliver, out_shape=(jax.ShapeDtypeStruct(spectral_state.sh...]
where the time goes in v2:
time: 243 us
  Pallas kernels  237 us (98%)
  local copies, waits for them, and re-layouts  3.41 us (1%)
    pallas_call x1, Pallas kernels, body(): pl.pallas_call(functools.partial(kernel, dims), out_shape=(jax.ShapeDtype...  232 us

profile of v2, /device:TPU:0, one launch (start us, length us, event | category | flops | bytes accessed | tf_op | source)
XLA Modules:
  0.0 242.7 jit_solution(3133862127373493413)
XLA Ops:
  0.6 0.7 convert_element_type.7
  1.3 0.7 select_maximum_fusion
  2.0 0.7 compare_select_fusion
  2.7 0.1 reshape.18
  2.8 0.1 tile.10
  2.9 232.3 %shard_map.86 = (f32[160,2,16,320]{3,2,1,0:T(8,128)}, bf16[4,160,2560]{2,1,0:T(8,128)(2,1)S(1)}) custom-call(f32[160,2,16,320]{3,2,1,0:T(8,128)} %state.1, bf16[160,2,16,320]{3,2,1,0:T(8,128)(2,1)} %noise.1, bf16[160,320,640]{2,1,0:T(8,128)(2,1)} %legendre.1, f32[1,1792]{1,0:T(1,128)S(1)} %reshape.17.small_in, s32[1,2048]{1,0:T(1,128)S(1)} %bitcast.4), custom_call_target="tpu_custom_call" | custom-call | tf_op jit(solution)/shard_map/pallas_call | solution.py:452
  235.2 0.0 copy-start
  235.2 3.2 %copy-done = f32[160,2,16,320]{3,2,1,0:T(8,128)S(1)} copy-done((f32[160,2,16,320]{3,2,1,0:T(8,128)S(1)}, f32[160,2,16,320]{3,2,1,0:T(8,128)}, u32[]{:S(2)}) %copy-start) | copy-done | bytes 6553624
  238.5 4.3 %shard_map.87 = (f32[160,2,16,320]{3,2,1,0:T(8,128)}, bf16[4,160,2560]{2,1,0:T(8,128)(2,1)}) custom-call(f32[160,2,16,320]{3,2,1,0:T(8,128)S(1)} %copy-done, bf16[4,160,2560]{2,1,0:T(8,128)(2,1)S(1)} %get-tuple-element.5.made_pattern), custom_call_target="tpu_custom_call" | custom-call | tf_op jit(solution)/shard_map/pallas_call | solution.py:469
  (6 shorter events, 0.0 us)
Async XLA Ops:
  235.2 3.2 %copy-start = (f32[160,2,16,320]{3,2,1,0:T(8,128)S(1)}, f32[160,2,16,320]{3,2,1,0:T(8,128)}, u32[]{:S(2)}) copy-start(f32[160,2,16,320]{3,2,1,0:T(8,128)} %get-tuple-element.4.made_state) | copy-start | bytes 19660804
